TPU v7x, 32 devices: a whole 2x2x4 slice. The times are simulated.
32 devices in a mesh: groups: 2 (over x), expert: 8 (over z, y), sub: 2 (over core).
Axes of the slice: x: 2, y: 2, z: 4, core: 2. Of those that a mesh axis runs over, the one named last changes fastest.
Arguments:
- hidden_state: bfloat16 [2048, 2048], P(('groups', 'expert', 'sub')), parts along dimension 0, may hold values from -6 to 6
- norm_gain: float32 [2048], replicated, may hold values from 0.5 to 1.5
- router_weight: bfloat16 [2048, 16], replicated, may hold values from -0.25 to 0.25
- expert_ids: int32 [2048, 6], P(('groups', 'expert', 'sub')), parts along dimension 0, may hold values from 0 to 15, all different within a row; in each aligned block of 64 rows (0 to 63, 64 to 127, ...) at most 32 rows name the same one
- live_counts: int32 [32], P(('groups', 'expert', 'sub')), parts along dimension 0, may hold values from 16 to 64
- routed_gate_up: bfloat16 [16, 2048, 2816], P(('expert', 'sub')), may hold values from -0.125 to 0.125
- routed_down: bfloat16 [16, 1408, 2048], P(('expert', 'sub')), may hold values from -0.15625 to 0.15625
- shared_weights: bfloat16 [3, 2048, 2816], P(None, None, 'expert'), may hold values from -0.125 to 0.125
Outputs:
- mixed: bfloat16 [2048, 2048], P(('groups', 'expert', 'sub')), parts along dimension 0
- penalty: float32 [2], P('groups'), parts along dimension 0
There are 2 independent parts, one for each index of `groups`. A program takes and returns all parts, laid end to end along the dimension named above; an argument that names none is the same for every part. Nothing has to cross between parts.
Inputs may be any that keep to these rules, and one draw needn't show every extreme that they name: `expert_ids`: in each row the 6 experts differ; among the 64 rows of one device no expert is named more than 32 times.
All inputs are finite; a program needn't handle non-finite values.
Results may differ from a plain program's by a relative error of at most 0.0065.
Values may be sent and summed in bfloat16 or wider, within the bound.
A program may use at most 128 MiB of HBM per device.

v0:
```python
import functools

import jax
import jax.numpy as jnp
from jax import lax
from jax.experimental import pallas as pl
from jax.experimental.pallas import tpu as pltpu
from jax.sharding import PartitionSpec as P

MESH = pl.DeviceIdType.MESH


def ring_place(chip, chips, fold):
    if fold == 1:
        return chip
    row, step = chip % 2, chip // 2
    return (1 - row) * step + row * (chips - 1 - step)


def ring_chip(place, chips, fold):
    if fold == 1:
        return place
    back = place // (chips // 2)
    step = (1 - back) * place + back * (chips - 1 - place)
    return 2 * step + back


def neighbours(chips, subs, fold):
    sub = lax.axis_index("sub")
    chip = lax.axis_index("expert")
    place = ring_place(chip, chips, fold)
    right = ring_chip((place + 1) % chips, chips, fold)
    left = ring_chip((place + chips - 1) % chips, chips, fold)
    along = [{"expert": right, "sub": sub}, {"expert": left, "sub": sub}]
    peers = [{"expert": chip, "sub": (sub + i) % subs} for i in range(1, subs)]
    return along, peers


def greet(along, peers):
    barrier = pltpu.get_barrier_semaphore()
    for target in along + peers:
        pl.semaphore_signal(barrier, inc=1, device_id=target, device_id_type=MESH)
    pl.semaphore_wait(barrier, len(along) + len(peers))


def carried(chips, hop, way, pieces):
    if 2 * hop < chips:
        return range(pieces)
    if 2 * hop == chips:
        return [0, 2] if way == 0 else [1]
    return []


def gather_kernel(
    chips, subs, fold, block_ref, notes_ref, all_ref, all_notes_ref,
    ring_send, ring_recv, peer_send, peer_recv, own_sem,
):
    along, peers = neighbours(chips, subs, fold)
    rows = block_ref.shape[0]
    half = rows // 2
    hops = chips // 2

    def piece(r, k, j):
        if j == 2:
            return all_notes_ref.at[r, k % chips]
        return all_ref.at[r, k % chips, pl.ds(j * half, half)]

    def own_piece(j):
        if j == 2:
            return notes_ref
        return block_ref.at[pl.ds(j * half, half)]

    def ring_copy(way, hop, j):
        sign = -1 if way == 0 else 1
        source = own_piece(j) if hop == 1 else piece(0, sign * (hop - 1), j)
        return pltpu.make_async_remote_copy(
            src_ref=source,
            dst_ref=piece(0, sign * hop, j),
            send_sem=ring_send.at[way, hop - 1, j],
            recv_sem=ring_recv.at[way, hop - 1, j],
            device_id=along[way],
            device_id_type=MESH,
        )

    def peer_copy(i, k, j):
        source = own_piece(j) if k == 0 else piece(0, k, j)
        return pltpu.make_async_remote_copy(
            src_ref=source,
            dst_ref=piece(subs - i, k, j),
            send_sem=peer_send.at[i - 1, k % chips, j],
            recv_sem=peer_recv.at[i - 1, k % chips, j],
            device_id=peers[i - 1],
            device_id_type=MESH,
        )

    keep = [
        pltpu.make_async_copy(block_ref, all_ref.at[0, 0], own_sem.at[0]),
        pltpu.make_async_copy(notes_ref, all_notes_ref.at[0, 0], own_sem.at[1]),
    ]
    greet(along, peers)
    started, pending = [], []
    for j in (2, 0, 1):
        for way in range(2):
            if j in carried(chips, 1, way, 3):
                copy = ring_copy(way, 1, j)
                copy.start()
                started.append(copy)
    for j in range(3):
        for i in range(1, subs):
            copy = peer_copy(i, 0, j)
            copy.start()
            started.append(copy)
            pending.append(copy)
    for copy in keep:
        copy.start()
    for hop in range(1, hops + 1):
        for j in (2, 0, 1):
            for way in range(2):
                if j not in carried(chips, hop, way, 3):
                    continue
                ring_copy(way, hop, j).wait_recv()
                if j in carried(chips, hop + 1, way, 3):
                    copy = ring_copy(way, hop + 1, j)
                    copy.start()
                    started.append(copy)
                for i in range(1, subs):
                    copy = peer_copy(i, -hop if way == 0 else hop, j)
                    copy.start()
                    started.append(copy)
                    pending.append(copy)
    for copy in pending:
        copy.wait_recv()
    for copy in started:
        copy.wait_send()
    for copy in keep:
        copy.wait()


def scatter_kernel(
    chips, subs, fold, *refs,
):
    parts = refs[:subs]
    out_ref, from_peer, going, coming, ring_send, ring_recv, peer_send, peer_recv = refs[subs:]
    along, peers = neighbours(chips, subs, fold)
    rows = out_ref.shape[0]
    half = rows // 2
    hops = chips // 2

    def peer_copy(i, k):
        k = k % chips
        return pltpu.make_async_remote_copy(
            src_ref=parts[i].at[k],
            dst_ref=from_peer.at[i - 1, k],
            send_sem=peer_send.at[i - 1, k],
            recv_sem=peer_recv.at[i - 1, k],
            device_id=peers[i - 1],
            device_id_type=MESH,
        )

    def ring_copy(way, hop, j):
        spot = (way, hop - 1, pl.ds(j * half, half))
        return pltpu.make_async_remote_copy(
            src_ref=going.at[spot],
            dst_ref=coming.at[spot],
            send_sem=ring_send.at[way, hop - 1, j],
            recv_sem=ring_recv.at[way, hop - 1, j],
            device_id=along[way],
            device_id_type=MESH,
        )

    def local_sum(k, j):
        span = pl.ds(j * half, half)
        value = parts[0][k % chips, span, :].astype(jnp.float32)
        for i in range(1, subs):
            value = value + from_peer[i - 1, k % chips, span, :].astype(jnp.float32)
        return value

    greet(along, peers)
    order = []
    for hop in range(hops, 0, -1):
        for k in (hop, -hop):
            if k % chips not in order:
                order.append(k % chips)
    order.append(0)
    sent = []
    for k in order:
        for i in range(1, subs):
            copy = peer_copy(i, k)
            copy.start()
            sent.append(copy)
    here = set()

    def need(k):
        if k % chips not in here:
            here.add(k % chips)
            for i in range(1, subs):
                peer_copy(i, k).wait_recv()

    for hop in range(hops, 0, -1):
        for j in range(2):
            for way in range(2):
                if j not in carried(chips, hop, way, 2):
                    continue
                k = hop if way == 0 else -hop
                need(k)
                value = local_sum(k, j)
                if j in carried(chips, hop + 1, way, 2):
                    ring_copy(way, hop + 1, j).wait_recv()
                    value = value + coming[way, hop, pl.ds(j * half, half), :].astype(jnp.float32)
                going[way, hop - 1, pl.ds(j * half, half), :] = value.astype(going.dtype)
                copy = ring_copy(way, hop, j)
                copy.start()
                sent.append(copy)
    need(0)
    for j in range(2):
        value = local_sum(0, j)
        for way in range(2):
            if j in carried(chips, 1, way, 2):
                ring_copy(way, 1, j).wait_recv()
                value = value + coming[way, 0, pl.ds(j * half, half), :].astype(jnp.float32)
        out_ref[pl.ds(j * half, half), :] = value.astype(out_ref.dtype)
    for copy in sent:
        copy.wait_send()


def ring_gather(block, notes, chips, subs, fold):
    hops = max(chips // 2, 1)
    vmem = pl.BlockSpec(memory_space=pltpu.VMEM)
    return pl.pallas_call(
        functools.partial(gather_kernel, chips, subs, fold),
        out_shape=(
            jax.ShapeDtypeStruct((subs, chips) + block.shape, block.dtype),
            jax.ShapeDtypeStruct((subs, chips) + notes.shape, notes.dtype),
        ),
        in_specs=[vmem, vmem],
        out_specs=(vmem, vmem),
        scratch_shapes=[
            pltpu.SemaphoreType.DMA((2, hops, 3)),
            pltpu.SemaphoreType.DMA((2, hops, 3)),
            pltpu.SemaphoreType.DMA((max(subs - 1, 1), chips, 3)),
            pltpu.SemaphoreType.DMA((max(subs - 1, 1), chips, 3)),
            pltpu.SemaphoreType.DMA((2,)),
        ],
        compiler_params=pltpu.CompilerParams(collective_id=0, has_side_effects=True),
        name="ring_gather",
    )(block, notes)


def ring_scatter(parts, chips, subs, fold):
    hops = max(chips // 2, 1)
    rows, width = parts[0].shape[1:]
    vmem = pl.BlockSpec(memory_space=pltpu.VMEM)
    return pl.pallas_call(
        functools.partial(scatter_kernel, chips, subs, fold),
        out_shape=jax.ShapeDtypeStruct((rows, width), parts[0].dtype),
        in_specs=[vmem] * subs,
        out_specs=vmem,
        scratch_shapes=[
            pltpu.VMEM((max(subs - 1, 1), chips, rows, width), parts[0].dtype),
            pltpu.VMEM((2, hops, rows, width), parts[0].dtype),
            pltpu.VMEM((2, hops, rows, width), parts[0].dtype),
            pltpu.SemaphoreType.DMA((2, hops, 2)),
            pltpu.SemaphoreType.DMA((2, hops, 2)),
            pltpu.SemaphoreType.DMA((max(subs - 1, 1), chips)),
            pltpu.SemaphoreType.DMA((max(subs - 1, 1), chips)),
        ],
        compiler_params=pltpu.CompilerParams(collective_id=1, has_side_effects=True),
        name="ring_scatter",
    )(*parts)


def normalize(states, norm_gain):
    values = states.astype(jnp.float32)
    spread = jnp.mean(values * values, axis=-1, keepdims=True)
    return (values * lax.rsqrt(spread + 1e-06) * norm_gain).astype(jnp.bfloat16)


def on_device(
    fold,
    hidden_state,
    norm_gain,
    router_weight,
    expert_ids,
    live_counts,
    routed_gate_up,
    routed_down,
    shared_weights,
):
    tok_rows, width = hidden_state.shape
    choose = expert_ids.shape[1]
    local_experts = routed_gate_up.shape[0]
    hidden_units = routed_down.shape[1]
    chips = lax.axis_size("expert")
    subs = lax.axis_size("sub")
    devices = chips * subs
    all_experts = local_experts * devices
    all_tokens = tok_rows * devices
    capacity = (tok_rows * choose * 4 + 3 * all_experts - 1) // (3 * all_experts)
    sub = lax.axis_index("sub")
    chip = lax.axis_index("expert")
    me = chip * subs + sub

    normed = normalize(hidden_state, norm_gain)
    probs = jax.nn.sigmoid(jnp.dot(normed, router_weight, preferred_element_type=jnp.float32))
    live = (jnp.arange(tok_rows, dtype=jnp.int32) < live_counts[0]).astype(jnp.float32)
    columns = jnp.arange(all_experts, dtype=jnp.int32)
    hot = jnp.sum((expert_ids[:, :, None] == columns[None, None, :]).astype(jnp.float32), axis=1)
    picked = hot * probs
    weights = live[:, None] * picked / jnp.sum(picked, axis=-1, keepdims=True)
    gate = probs * live[:, None]
    high = gate.astype(jnp.bfloat16)
    low = (gate - high.astype(jnp.float32)).astype(jnp.bfloat16)
    notes = jnp.concatenate(
        [weights.astype(jnp.bfloat16), (hot * live[:, None]).astype(jnp.bfloat16), high, low], axis=-1
    )
    spare = -notes.shape[1] % 128
    notes = jnp.pad(notes, ((0, 0), (0, spare)))
    everyone, notes = ring_gather(normed, notes, chips, subs, fold)

    notes = notes.astype(jnp.float32)
    place = ring_place(chip, chips, fold)
    origin = (
        ring_chip((place + jnp.arange(chips)[None, :]) % chips, chips, fold) * subs
        + (sub + jnp.arange(subs)[:, None]) % subs
    ).reshape(devices)
    sums = jnp.sum(notes.reshape(devices, tok_rows, -1), axis=1)
    at = origin[None, :] == jnp.arange(devices)[:, None]
    sums = jnp.sum(jnp.where(at[:, :, None], sums[None], 0.0), axis=1)
    sums = jnp.sum(sums, axis=0)
    load = sums[all_experts : 2 * all_experts]
    mass = sums[2 * all_experts : 3 * all_experts] + sums[3 * all_experts : 4 * all_experts]
    penalty = all_experts * jnp.sum(load * mass) / (choose * float(all_tokens) * float(all_tokens))

    span = chips * tok_rows
    slots = chips * capacity
    everyone = everyone.reshape(subs, span, width)
    notes = notes.reshape(subs, span, -1)
    lanes = jnp.arange(notes.shape[2])
    owner = jnp.arange(span, dtype=jnp.int32) // tok_rows
    cells = jnp.arange(slots, dtype=jnp.int32)
    before = (jnp.arange(tok_rows)[:, None] < jnp.arange(tok_rows)[None, :]).astype(jnp.float32)
    mixed = [0.0] * subs
    for item in range(local_experts):
        column = me * local_experts + item
        weight = jnp.sum(jnp.where(lanes == column, notes, 0.0), axis=2)
        chosen = jnp.sum(jnp.where(lanes == all_experts + column, notes, 0.0), axis=2)
        rank = jnp.dot(chosen.reshape(devices, tok_rows), before).reshape(subs, span)
        spot = jnp.where(chosen > 0, rank.astype(jnp.int32) + owner * capacity, -1)
        match = spot[:, :, None] == cells
        table = match.astype(jnp.bfloat16)
        mixing = jnp.where(match, weight[:, :, None], 0.0).astype(jnp.bfloat16)
        table, mixing = lax.optimization_barrier((table, mixing))
        rows = lax.dot_general(
            table, everyone, (((1,), (1,)), ((0,), (0,))), preferred_element_type=jnp.float32
        ).astype(jnp.bfloat16).reshape(subs * slots, width)
        rows = lax.optimization_barrier(rows)
        inner = jnp.dot(rows, routed_gate_up[item], preferred_element_type=jnp.float32)
        active = (jax.nn.silu(inner[:, :hidden_units]) * inner[:, hidden_units:]).astype(
            jnp.bfloat16
        )
        active = lax.optimization_barrier(active)
        results = jnp.dot(active, routed_down[item], preferred_element_type=jnp.float32).astype(
            jnp.bfloat16
        )
        results = lax.optimization_barrier(results)
        for r in range(subs):
            mixed[r] = mixed[r] + jnp.dot(
                mixing[r], results[r * slots : (r + 1) * slots], preferred_element_type=jnp.float32
            )

    piece = everyone[0]
    gate_part = jnp.dot(piece, shared_weights[0], preferred_element_type=jnp.float32)
    up_part = jnp.dot(piece, shared_weights[1], preferred_element_type=jnp.float32)
    shared_active = (jax.nn.silu(gate_part) * up_part).astype(jnp.bfloat16)
    shared_active = lax.optimization_barrier(shared_active)
    partials = lax.dot_general(
        shared_active,
        shared_weights[2],
        (((1,), (1,)), ((), ())),
        preferred_element_type=jnp.float32,
    )
    mixed[0] = mixed[0] + partials
    parts = [part.astype(jnp.bfloat16).reshape(chips, tok_rows, width) for part in mixed]
    return (ring_scatter(parts, chips, subs, fold), penalty.reshape(1))


def fold_of(mesh):
    chips = mesh.shape["expert"]
    try:
        spots = [tuple(d.coords) for d in mesh.devices[0, :, 0].flat]
    except (AttributeError, TypeError, ValueError):
        spots = []
    if chips % 2 or chips < 4:
        return 1
    if len(spots) == chips:
        apart = sum(abs(a - b) for a, b in zip(spots[0], spots[2]))
        return 2 if apart == 1 else 1
    return 1


def solution(mesh):
    placed = (
        P(("groups", "expert", "sub"), None),
        P(),
        P(),
        P(("groups", "expert", "sub"), None),
        P(("groups", "expert", "sub")),
        P(("expert", "sub"), None, None),
        P(("expert", "sub"), None, None),
        P(None, None, "expert"),
    )
    return jax.shard_map(
        functools.partial(on_device, fold_of(mesh)),
        mesh=mesh,
        in_specs=placed,
        out_specs=(P(("groups", "expert", "sub"), None), P("groups")),
        check_vma=False,
    )
```

profile of v0, /device:TPU:0, one launch (start us, length us, event | category | flops | bytes accessed | tf_op | source)
XLA Modules:
  0.0 99.8 jit_solution(1035824712889063030)
XLA Ops:
  1.4 0.1 add.166
  1.5 1.1 %fusion.29 = f32[64]{0:T(128)S(1)} fusion(bf16[64,2048]{1,0:T(8,128)(2,1)} %param.8), kind=kLoop, calls=%fused_computation.36 | loop fusion | flops 393152 | bytes 262400 | tf_op jit(solution)/shard_map/reduce_sum | solution.py:274
  2.7 0.7 convert_reduce_fusion.1
  3.4 0.1 copy.16
  3.5 1.1 %fusion.31.block_ref = bf16[64,2048]{1,0:T(8,128)(2,1)S(1)} fusion(bf16[64,2048]{1,0:T(8,128)(2,1)} %param.8, f32[2048]{0:T(1024)} %param.9, f32[64]{0:T(128)S(1)} %add_rsqrt_fusion), kind=kLoop, calls=%fused_computation.38 | loop fusion | flops 524288 | bytes 532736 | tf_op jit(solution)/shard_map/convert_element_type | solution.py:275
  4.6 0.3 multiply_reduce_fusion
  4.9 0.1 divide_convert_fusion
  5.0 0.7 fusion.44.notes_ref
  5.7 32.3 %ring_gather.1 = (bf16[2,8,64,2048]{3,2,1,0:T(8,128)(2,1)}, bf16[2,8,64,128]{3,2,1,0:T(8,128)(2,1)}) custom-call(bf16[64,2048]{1,0:T(8,128)(2,1)} %copy-done.2, bf16[64,128]{1,0:T(8,128)(2,1)} %fusion.44.notes_ref), custom_call_target="tpu_custom_call" | custom-call | tf_op jit(solution)/shard_map/ring_gather/pallas_call | solution.py:229
  38.0 1.3 %convert_reduce_fusion = (f32[2,8,128]{2,1,0:T(8,128)S(1)}, bf16[2,8,64]{2,1,0:T(8,128)(2,1)S(1)}, f32[2,8,64]{2,1,0:T(8,128)S(1)}) fusion(bf16[2,8,64,128]{3,2,1,0:T(8,128)(2,1)} %get-tuple-element.6, pred[128]{0:T(512)(128)(4,1)S(1)} %get-tuple-element.19, pred[128]{0:T(512)(128)(4,1)S(1)} %get-tuple-element.20), kind=kLoop, calls=%fused_computation.31 | loop fusion | flops 782336 | bytes 276736 | tf_op jit(solution)/shard_map/reduce_sum | solution.py:326
  39.3 0.1 select_reduce_fusion
  39.4 0.7 multiply_reduce_fusion.1
  40.8 0.1 broadcast_in_dim.75
  40.9 0.1 convolution_convert_fusion.2
  41.1 0.1 gt.15
  41.2 0.2 select_convert_fusion
  41.3 0.1 fusion.28
  41.5 3.6 %convolution_convert_fusion.1 = bf16[2,256,2048]{2,1,0:T(8,128)(2,1)S(1)} fusion(bf16[2,512,256]{1,2,0:T(8,128)(2,1)S(1)} %fusion.28, bf16[2,512,2048]{2,1,0:T(8,128)(2,1)} %bitcast.57), kind=kOutput, calls=%fused_computation.6 | convolution fusion | flops 1074790400 | bytes 6815744 | tf_op jit(solution)/shard_map/dot_general | solution.py:353
  45.1 0.2 slice.44
  45.4 0.9 copy-done.3
  46.2 0.9 fusion.11
  47.2 1.0 fusion.19
  48.2 0.6 slice-done.1
  48.8 1.0 slice-done.2
  49.8 6.2 %fusion = f32[512,2816]{1,0:T(8,128)S(1)} fusion(bf16[512,2048]{1,0:T(8,128)(2,1)S(1)} %bitcast.60, bf16[1,2048,2816]{2,1,0:T(8,128)(2,1)S(1)} %bitcast.65), kind=kOutput, calls=%fused_computation | convolution fusion | flops 5905580032 | bytes 19398656 | tf_op jit(solution)/shard_map/dot_general | solution.py:357
  56.0 0.9 fusion.7
  56.8 3.8 %fusion.4 = bf16[512,2048]{1,0:T(8,128)(2,1)S(1)} fusion(bf16[512,1408]{1,0:T(8,128)(2,1)S(1)} %fusion.7, bf16[1,1408,2048]{2,1,0:T(8,128)(2,1)S(1)} %bitcast.67), kind=kOutput, calls=%fused_computation.7 | convolution fusion | flops 2953838592 | bytes 9306112 | tf_op jit(solution)/shard_map/dot_general | solution.py:362
  60.7 2.0 %convolution_convert_fusion = bf16[512,2048]{1,0:T(8,128)(2,1)} fusion(bf16[512,2048]{1,0:T(8,128)(2,1)S(1)} %fusion.4, bf16[2,512,256]{1,2,0:T(8,128)(2,1)S(1)} %select_convert_fusion), kind=kOutput, calls=%fused_computation.5 | convolution fusion | flops 537919488 | bytes 3407872 | tf_op jit(solution)/shard_map/dot_general | solution.py:367
  62.7 0.7 fusion.26
  63.4 2.7 %add_convert_fusion = bf16[512,2048]{1,0:T(8,128)(2,1)} fusion(f32[512,2048]{1,0:T(8,128)S(1)} %fusion.26, bf16[512,352]{0,1:T(8,128)(2,1)S(1)} %fusion.19, bf16[3,2048,352]{1,2,0:T(8,128)(2,1)S(1)} %copy-done.3), kind=kOutput, calls=%fused_computation.4 | convolution fusion | flops 740294656 | bytes 8093696 | tf_op jit(solution)/shard_map/dot_general | solution.py:376
  66.2 30.8 %ring_scatter.1 = bf16[64,2048]{1,0:T(8,128)(2,1)} custom-call(bf16[8,64,2048]{2,1,0:T(8,128)(2,1)} %bitcast.59, bf16[8,64,2048]{2,1,0:T(8,128)(2,1)} %bitcast.58), custom_call_target="tpu_custom_call" | custom-call | tf_op jit(solution)/shard_map/ring_scatter/pallas_call | solution.py:253
  97.0 1.7 %copy.24 = bf16[64,2048]{1,0:T(8,128)(2,1)} copy(bf16[64,2048]{1,0:T(8,128)(2,1)} %ring_scatter.1) | data formatting | bytes 524288
  (28 shorter events, 0.3 us)
Async XLA Ops:
  0.6 3.9 %copy-start = (bf16[2048,16]{0,1:T(8,128)(2,1)S(1)}, bf16[2048,16]{0,1:T(8,128)(2,1)}, u32[]{:S(2)}) copy-start(bf16[2048,16]{0,1:T(8,128)(2,1)} %param.10) | copy-start | bytes 196612
  4.6 1.1 %copy-start.2 = (bf16[64,2048]{1,0:T(8,128)(2,1)}, bf16[64,2048]{1,0:T(8,128)(2,1)S(1)}, u32[]{:S(2)}) copy-start(bf16[64,2048]{1,0:T(8,128)(2,1)S(1)} %fusion.31.block_ref) | copy-start | bytes 786436
  41.5 3.6 %copy-start.1 = (bf16[2,8,64,2048]{3,2,1,0:T(8,128)(2,1)S(1)}, bf16[2,8,64,2048]{3,2,1,0:T(8,128)(2,1)}, u32[]{:S(2)}) copy-start(bf16[2,8,64,2048]{3,2,1,0:T(8,128)(2,1)} %get-tuple-element.9) | copy-start | bytes 12582916
  41.5 4.8 %copy-start.3 = (bf16[3,2048,352]{1,2,0:T(8,128)(2,1)S(1)}, bf16[3,2048,352]{1,2,0:T(8,128)(2,1)}, u32[]{:S(2)}) copy-start(bf16[3,2048,352]{1,2,0:T(8,128)(2,1)} %param.15) | copy-start | bytes 12976132
  45.1 3.1 %slice-start = ((s8[11534336]{0:T(1024)(128)(4,1)}), s8[4194304]{0:T(1024)(128)(4,1)S(1)}, s32[]{:S(2)}) async-start(s8[11534336]{0:T(1024)(128)(4,1)} %bitcast.64), calls=%async_computation | async-start | bytes 8388608
  46.2 2.6 %slice-start.1 = ((s8[11534336]{0:T(1024)(128)(4,1)}), s8[4194304]{0:T(1024)(128)(4,1)S(1)}, s32[]{:S(2)}) async-start(s8[11534336]{0:T(1024)(128)(4,1)} %bitcast.64), calls=%async_computation.1 | async-start | bytes 8388608
  47.2 2.6 %slice-start.2 = ((s8[11534336]{0:T(1024)(128)(4,1)}), s8[3145728]{0:T(1024)(128)(4,1)S(1)}, s32[]{:S(2)}) async-start(s8[11534336]{0:T(1024)(128)(4,1)} %bitcast.64), calls=%async_computation.2 | async-start | bytes 6291456
  47.2 9.6 %slice-start.3 = ((s8[5767168]{0:T(1024)(128)(4,1)}), s8[4194304]{0:T(1024)(128)(4,1)S(1)}, s32[]{:S(2)}) async-start(s8[5767168]{0:T(1024)(128)(4,1)} %bitcast.66), calls=%async_computation.3 | async-start | bytes 8388608
  49.8 7.1 %slice-start.4 = ((s8[5767168]{0:T(1024)(128)(4,1)}), s8[1572864]{0:T(1024)(128)(4,1)S(1)}, s32[]{:S(2)}) async-start(s8[5767168]{0:T(1024)(128)(4,1)} %bitcast.66), calls=%async_computation.4 | async-start | bytes 3145728
where the time goes:
time: 100 us; the launch traced here: 99.8 us
  Pallas kernels  63.1 us (63%)
  matrix products  21.5 us (22%)
  other arithmetic  7.06 us (7%)
  local copies, waits for them, and re-layouts  4.79 us (5%)
  between operations  3.34 us (3%)
    pallas_call x1, Pallas kernels, ring_gather(): pl.pallas_call(functools.partial(gather_kernel, chips, subs, fold), out_s...  32.3 us
    pallas_call x1, Pallas kernels, ring_scatter(): pl.pallas_call(functools.partial(scatter_kernel, chips, subs, fold), out_...  30.8 us
    dot_general x1, matrix products, on_device(): jnp.dot(rows, routed_gate_up[item], preferred_element_type=jnp.float32)  6.2 us
    unnamed x19, local copies, waits for them, and re-layouts  4.14 us
    dot_general x1, matrix products, on_device(): jnp.dot(active, routed_down[item], preferred_element_type=jnp.float32)  3.81 us
    dot_general x1, matrix products, on_device(): lax.dot_general(table, everyone, (((1,), (1,)), ((0,), (0,))), preferred_...  3.6 us
    dot_general x2, matrix products, on_device(): jnp.dot(mixing[r], results[r * slots:(r + 1) * slots], preferred_element_...  2.79 us
    dot_general x1, matrix products, on_device(): lax.dot_general(shared_active, shared_weights[2], (((1,), (1,)), ((), ())...  2.73 us

commit v1 on v0

v1 whole, which is shorter than its diff:
```python
import functools

import jax
import jax.numpy as jnp
from jax import lax
from jax.experimental import pallas as pl
from jax.experimental.pallas import tpu as pltpu
from jax.sharding import PartitionSpec as P

MESH = pl.DeviceIdType.MESH
LANES = 128
SLOTS = 5


def ring_place(chip, chips, fold):
    if fold == 1:
        return chip
    row, step = chip % 2, chip // 2
    return (1 - row) * step + row * (chips - 1 - step)


def ring_chip(place, chips, fold):
    if fold == 1:
        return place
    back = place // (chips // 2)
    step = (1 - back) * place + back * (chips - 1 - place)
    return 2 * step + back


class Plan:
    def __init__(self, chips, fold, tok, width, units, shared, choose, experts):
        self.chips, self.fold, self.hops = chips, fold, chips // 2
        self.tok, self.width, self.half = tok, width, tok // 2
        self.units, self.shared, self.choose, self.experts = units, shared, choose, experts
        self.sublanes = -(-experts // 16) * 16
        hops = self.hops
        order = [(0, 0), (0, 1)]
        for hop, j in (
            [(1, 0), (1, 1)]
            + [(h, 0) for h in range(2, hops + 1)]
            + [(h, 1) for h in range(2, hops + 1)]
        ):
            order.append((hop, j))
            if hop < hops:
                order.append((chips - hop, j))
        self.order = order
        self.group = 4
        self.steps = len(order) // self.group
        self.rows = self.group * 2 * self.half
        self.routed_tiles = units // LANES
        full = shared // LANES
        self.pairs = full // 2
        self.rest = [
            (at, min(LANES, shared - at)) for at in range(self.pairs * 2 * LANES, shared, LANES)
        ]
        self.tiles = self.routed_tiles + self.pairs + len(self.rest)
        self.depth = self.tiles * LANES
        self.downs = width // 256

    def index(self, k, j):
        return self.order.index((k % self.chips, j))

    def span(self, r, k, j):
        return pl.ds((2 * self.index(k, j) + r) * self.half, self.half)

    def cols(self, c):
        return pl.ds(c * (self.width // 2), self.width // 2)

    def step_of(self, k, j):
        return self.index(k, j) // self.group


def silu(v):
    return v / (1.0 + jnp.exp(-v))


def layer_kernel(
    plan, hid_hbm, gain_hbm, router_hbm, ids_hbm, live_ref, gu_hbm, dn_hbm, sh_hbm,
    out_ref, pen_ref,
    hid, gain, router, ids, square, notes, wt, wd, stage, x_all, y_all, from_peer, going, coming,
    act, rbuf, scale, in_sem, w_sem, gs, gr, ps, pr, ys, yr, ss, sr,
):
    chips, fold, hops, half = plan.chips, plan.fold, plan.hops, plan.half
    tok, width, tiles = plan.tok, plan.width, plan.tiles
    sub = lax.axis_index("sub")
    chip = lax.axis_index("expert")
    me = chip * 2 + sub
    place = ring_place(chip, chips, fold)
    right = ring_chip((place + 1) % chips, chips, fold)
    left = ring_chip((place + chips - 1) % chips, chips, fold)
    along = [{"expert": right, "sub": sub}, {"expert": left, "sub": sub}]
    peer = {"expert": chip, "sub": 1 - sub}
    sign = (-1, 1)

    def remote(src, dst, send, recv, device):
        return pltpu.make_async_remote_copy(
            src_ref=src, dst_ref=dst, send_sem=send, recv_sem=recv,
            device_id=device, device_id_type=MESH,
        )

    def gather_copy(way, hop, j):
        cols = plan.cols(way) if hop == hops else pl.ds(0, width)
        src = x_all.at[plan.span(0, sign[way] * (hop - 1), j), cols]
        dst = x_all.at[plan.span(0, sign[way] * hop, j), cols]
        return remote(src, dst, gs.at[way, hop - 1, j], gr.at[way, hop - 1, j], along[way])

    def note_copy(way, hop):
        src = notes.at[0, sign[way] * (hop - 1) % chips]
        dst = notes.at[0, sign[way] * hop % chips]
        return remote(src, dst, gs.at[way, hop - 1, 2], gr.at[way, hop - 1, 2], along[way])

    def peer_copies(k, j):
        k = k % chips
        parts = (0, 1) if k == hops else (2,)
        made = []
        for c in parts:
            cols = pl.ds(0, width) if c == 2 else plan.cols(c)
            at = 2 * j + c % 2
            made.append(
                remote(
                    x_all.at[plan.span(0, k, j), cols], x_all.at[plan.span(1, k, j), cols],
                    ps.at[k, at], pr.at[k, at], peer,
                )
            )
        return made

    def peer_note(k):
        k = k % chips
        return remote(notes.at[0, k], notes.at[1, k], ps.at[k, 4], pr.at[k, 4], peer)

    def part_copy(q, c):
        cols = plan.cols(c)
        if isinstance(q, int):
            src, dst = pl.ds((2 * q + 1) * half, half), pl.ds(q * half, half)
        else:
            src = pl.ds(pl.multiple_of((2 * q + 1) * half, half), half)
            dst = pl.ds(pl.multiple_of(q * half, half), half)
        return remote(
            y_all.at[src, cols], from_peer.at[dst, cols], ys.at[q, c], yr.at[q, c], peer
        )

    def sum_copy(way, hop, j, c):
        spot = (way, hop - 1, pl.ds(j * half, half), plan.cols(c))
        at = 2 * j + c
        return remote(
            going.at[spot], coming.at[spot], ss.at[way, hop - 1, at], sr.at[way, hop - 1, at],
            along[way],
        )

    def ways_of(hop, c):
        return (c,) if hop == hops else (0, 1)

    small = [
        pltpu.make_async_copy(hid_hbm, hid, in_sem.at[0]),
        pltpu.make_async_copy(gain_hbm, gain, in_sem.at[1]),
        pltpu.make_async_copy(router_hbm, router, in_sem.at[2]),
        pltpu.make_async_copy(ids_hbm, ids, in_sem.at[3]),
        pltpu.make_async_copy(sh_hbm, stage, in_sem.at[4]),
    ]
    down_load = pltpu.make_async_copy(dn_hbm.at[0], wd.at[pl.ds(0, plan.units)], in_sem.at[5])

    def tile_loads(n):
        if n < plan.routed_tiles:
            return [
                pltpu.make_async_copy(
                    gu_hbm.at[0, :, pl.ds(side * plan.units + n * LANES, LANES)],
                    wt.at[n, :, pl.ds(side * LANES, LANES)], w_sem.at[n, side],
                )
                for side in range(2)
            ]
        return []

    for copy in small[:4]:
        copy.start()
    barrier = pltpu.get_barrier_semaphore()
    for target in along + [peer]:
        pl.semaphore_signal(barrier, inc=1, device_id=target, device_id_type=MESH)
    small[4].start()
    for n in range(tiles):
        for copy in tile_loads(n):
            copy.start()
    down_load.start()

    small[0].wait()
    small[1].wait()
    for j in range(2):
        values = hid[pl.ds(j * half, half), :].astype(jnp.float32)
        spread = jnp.mean(values * values, axis=-1, keepdims=True)
        x_all[plan.span(0, 0, j), :] = (
            values * lax.rsqrt(spread + 1e-06) * gain[...]
        ).astype(jnp.bfloat16)
    pl.semaphore_wait(barrier, 3)
    for way in range(2):
        if hops > 1 or way == 0:
            gather_copy(way, 1, 0).start()
    for copy in peer_copies(0, 0):
        copy.start()

    small[2].wait()
    small[3].wait()
    experts = plan.experts
    columns = lax.broadcasted_iota(jnp.int32, (half, experts), 1)
    square[...] = jnp.zeros_like(square)
    load = jnp.zeros((1, experts), jnp.float32)
    mass = jnp.zeros((1, experts), jnp.float32)
    for j in range(2):
        normed = x_all[plan.span(0, 0, j), :]
        logits = jnp.dot(normed, router[...], preferred_element_type=jnp.float32)
        probs = 1.0 / (1.0 + jnp.exp(-logits))
        named = ids[pl.ds(j * half, half), :]
        hot = jnp.zeros((half, experts), jnp.float32)
        for k in range(plan.choose):
            hot = hot + jnp.where(named[:, k : k + 1] == columns, 1.0, 0.0)
        token = lax.broadcasted_iota(jnp.int32, (half, experts), 0) + j * half
        live = jnp.where(token < live_ref[0], 1.0, 0.0)
        picked = hot * probs
        weights = live * picked / jnp.sum(picked, axis=-1, keepdims=True)
        square[pl.ds(j * half, half), pl.ds(0, experts)] = weights
        load = load + jnp.sum(hot * live, axis=0, keepdims=True)
        mass = mass + jnp.sum(probs * live, axis=0, keepdims=True)
    square[pl.ds(tok, 1), pl.ds(0, experts)] = load
    for at in range(3):
        kept = mass.astype(jnp.bfloat16).astype(jnp.float32)
        square[pl.ds(tok + 1 + at, 1), pl.ds(0, experts)] = kept
        mass = mass - kept
    turned = jnp.transpose(square[...])
    notes[0, 0] = turned[: plan.sublanes].astype(jnp.bfloat16)
    for way in range(2):
        if hops > 1 or way == 0:
            note_copy(way, 1).start()
        if hops > 1 or way == 1:
            gather_copy(way, 1, 1).start()
    peer_note(0).start()
    for copy in peer_copies(0, 1):
        copy.start()

    small[4].wait()
    for i in range(plan.pairs):
        lanes = pl.ds(pl.multiple_of((2 * i + sub) * LANES, LANES), LANES)
        n = plan.routed_tiles + i
        for side in range(2):
            wt[n, :, pl.ds(side * LANES, LANES)] = stage[side, :, lanes]
        wd[pl.ds(n * LANES, LANES), :] = jnp.transpose(stage[2, :, lanes])
    for i, (at, wide) in enumerate(plan.rest):
        n = plan.routed_tiles + plan.pairs + i
        if wide < LANES:
            wt[n] = jnp.zeros_like(wt[n])
        for side in range(2):
            wt[n, :, pl.ds(side * LANES, wide)] = stage[side, :, pl.ds(at, wide)]
        wd[pl.ds(n * LANES, wide), :] = jnp.transpose(stage[2, :, pl.ds(at, wide)])
        if wide < LANES:
            wd[pl.ds(n * LANES + wide, LANES - wide), :] = jnp.zeros(
                (LANES - wide, width), jnp.bfloat16
            )

    events = {}

    def at_slot(spot, event):
        events.setdefault(spot, []).append(event)

    def arrive(hop, j):
        for way in range(2):
            k = sign[way] * hop
            if j == 0 and (hop < hops or way == 0):
                note_copy(way, hop).wait_recv()
                if hop + 1 < hops or (hop + 1 == hops and way == 0):
                    note_copy(way, hop + 1).start()
                peer_note(k).start()
            gather_copy(way, hop, j).wait_recv()
            if hop + 1 <= hops:
                gather_copy(way, hop + 1, j).start()
            made = peer_copies(k, j)
            (made[way] if hop == hops else made[0]).start()

    def ready(step):
        for i in range(plan.group):
            k, j = plan.order[step * plan.group + i]
            for copy in peer_copies(k, j):
                copy.wait_recv()
            if j == 0:
                peer_note(k).wait_recv()
            for r in range(2):
                tile = notes[r, k].astype(jnp.float32)
                mine = lax.broadcasted_iota(jnp.int32, tile.shape, 0) == me
                line = jnp.sum(jnp.where(mine, tile, 0.0), axis=0, keepdims=True)
                row = lax.broadcasted_iota(jnp.int32, (half, LANES), 0) + j * half
                lane = lax.broadcasted_iota(jnp.int32, (half, LANES), 1)
                column = jnp.sum(jnp.where(row == lane, line, 0.0), axis=1, keepdims=True)
                scale[pl.ds((2 * i + r) * half, half), :] = jnp.broadcast_to(column, (half, LANES))

    arrivals = [(h, j) for h in range(1, hops + 1) for j in range(2)]
    wanted = [0, 1, 3, 6, 8, 10, 10, 11]
    spots = []
    for i, (hop, j) in enumerate(arrivals):
        due = SLOTS * min(plan.step_of(hop, j), plan.step_of(-hop, j))
        spots.append(min(due, wanted[i] if i < len(wanted) else 2 * i))
    for i in reversed(range(len(spots) - 1)):
        spots[i] = min(spots[i], spots[i + 1])
    for (hop, j), spot in zip(arrivals, spots):
        at_slot(spot, functools.partial(arrive, hop, j))
    for step in range(plan.steps):
        at_slot(SLOTS * step, functools.partial(ready, step))
    quarter = 4

    def loads(first, last):
        for n in range(first, min(last, tiles)):
            for copy in tile_loads(n):
                copy.wait()

    for part in range(3):
        last = tiles if part == 2 else quarter * (part + 1)
        at_slot(part, functools.partial(loads, quarter * part, last))
    at_slot(2, down_load.wait)

    def own_part(k, j, c):
        q = plan.index(k, j)
        part_copy(q, c).wait_recv()
        value = y_all[plan.span(0, k, j), plan.cols(c)].astype(jnp.float32)
        return value + from_peer[pl.ds(q * half, half), plan.cols(c)].astype(jnp.float32)

    def pass_on(hop, j):
        for c in range(2):
            shared = None
            for way in ways_of(hop, c):
                k = -sign[way] * hop
                value = own_part(k, j, c)
                if hop < hops and way in ways_of(hop + 1, c):
                    sum_copy(way, hop + 1, j, c).wait_recv()
                    spot = (way, hop, pl.ds(j * half, half), plan.cols(c))
                    value = value + coming[spot].astype(jnp.float32)
                spot = (way, hop - 1, pl.ds(j * half, half), plan.cols(c))
                going[spot] = value.astype(going.dtype)
                sum_copy(way, hop, j, c).start()

    def finish(j):
        for c in range(2):
            value = own_part(0, j, c)
            for way in ways_of(1, c):
                sum_copy(way, 1, j, c).wait_recv()
                spot = (way, 0, pl.ds(j * half, half), plan.cols(c))
                value = value + coming[spot].astype(jnp.float32)
            out_ref[pl.ds(j * half, half), plan.cols(c)] = value.astype(out_ref.dtype)

    first = [functools.partial(pass_on, h, 0) for h in range(hops, 0, -1)]
    first.append(functools.partial(finish, 0))
    second = [functools.partial(pass_on, h, 1) for h in range(hops, 0, -1)]
    second.append(functools.partial(finish, 1))
    spot = SLOTS * (plan.step_of(hops, 0) + 1) + 1
    while EARLY and spot < SLOTS * plan.steps and len(first) > 1:
        at_slot(spot, first.pop(0))
        spot += 3

    def run(t, slot):
        for step in range(plan.steps):
            todo = events.get(SLOTS * step + slot, [])
            if todo:

                @pl.when(t == step)
                def _():
                    for event in todo:
                        event()

    own_row = (lax.broadcasted_iota(jnp.int32, (plan.rows, LANES), 0) // half) % 2 == 0
    lane = lax.broadcasted_iota(jnp.int32, (plan.rows, LANES), 1)

    def activate(n):
        both = rbuf[...]
        value = silu(both[:, :LANES]) * both[:, LANES:]
        if n < plan.routed_tiles:
            value = value * scale[...]
        elif n >= plan.routed_tiles + plan.pairs:
            wide = plan.rest[n - plan.routed_tiles - plan.pairs][1]
            value = jnp.where(own_row & (lane < wide), value, 0.0)
        act[:, pl.ds(n * LANES, LANES)] = value.astype(jnp.bfloat16)

    def step_body(t, carry):
        rows = pl.ds(pl.multiple_of(t * plan.rows, plan.rows), plan.rows)
        run(t, 0)
        for n in range(tiles):
            if n > 0:
                activate(n - 1)
            rbuf[...] = jnp.dot(x_all[rows, :], wt[n], preferred_element_type=jnp.float32)
            if (n + 1) % quarter == 0 and (n + 1) // quarter < SLOTS - 1:
                run(t, (n + 1) // quarter)
        activate(tiles - 1)
        for n in range(plan.downs):
            cols = pl.ds(n * 256, 256)
            y_all[rows, cols] = jnp.dot(
                act[...], wd[:, cols], preferred_element_type=jnp.float32
            ).astype(jnp.bfloat16)
            if 2 * (n + 1) == plan.downs:
                for i in range(plan.group):
                    part_copy(plan.group * t + i, 0).start()
                run(t, SLOTS - 1)
        for i in range(plan.group):
            part_copy(plan.group * t + i, 1).start()
        return carry

    lax.fori_loop(0, plan.steps, step_body, 0)

    while first or second:
        if second and len(second) >= len(first):
            second.pop(0)()
        else:
            first.pop(0)()

    total = jnp.zeros((plan.sublanes, LANES), jnp.float32)
    for r in range(2):
        for k in range(chips):
            total = total + notes[r, k].astype(jnp.float32)
    mass = total[:, tok + 1 : tok + 2] + total[:, tok + 2 : tok + 3] + total[:, tok + 3 : tok + 4]
    every = float(tok * chips * 2)
    penalty = experts * jnp.sum(total[:, tok : tok + 1] * mass) / (plan.choose * every * every)
    pen_ref[0] = penalty

    for hop in range(1, hops + 1):
        for way in range(2):
            for j in range(2):
                gather_copy(way, hop, j).wait_send()
            if hop < hops or way == 0:
                note_copy(way, hop).wait_send()
            for j in range(2):
                for c in range(2):
                    if way in ways_of(hop, c):
                        sum_copy(way, hop, j, c).wait_send()
    for k in range(chips):
        peer_note(k).wait_send()
        for j in range(2):
            for copy in peer_copies(k, j):
                copy.wait_send()
    for q in range(len(plan.order)):
        for c in range(2):
            part_copy(q, c).wait_send()


EARLY = True


def on_device(
    fold, hidden_state, norm_gain, router_weight, expert_ids, live_counts,
    routed_gate_up, routed_down, shared_weights,
):
    tok, width = hidden_state.shape
    chips, subs = lax.axis_size("expert"), lax.axis_size("sub")
    units, shared = routed_down.shape[1], shared_weights.shape[2]
    if subs != 2 or chips % 4 or routed_gate_up.shape[0] != 1 or tok + 4 > LANES:
        raise ValueError("unsupported sizes")
    plan = Plan(
        chips, fold, tok, width, units, shared, expert_ids.shape[1], router_weight.shape[1]
    )
    hops, count = plan.hops, len(plan.order)
    bf16, f32 = jnp.bfloat16, jnp.float32
    hbm = pl.BlockSpec(memory_space=pl.ANY)
    dma = pltpu.SemaphoreType.DMA
    mixed, penalty = pl.pallas_call(
        functools.partial(layer_kernel, plan),
        out_shape=(
            jax.ShapeDtypeStruct((tok, width), bf16),
            jax.ShapeDtypeStruct((1,), f32),
        ),
        in_specs=[hbm] * 4 + [pl.BlockSpec(memory_space=pltpu.SMEM)] + [hbm] * 3,
        out_specs=(
            pl.BlockSpec(memory_space=pltpu.VMEM),
            pl.BlockSpec(memory_space=pltpu.SMEM),
        ),
        scratch_shapes=[
            pltpu.VMEM((tok, width), bf16),
            pltpu.VMEM((1, width), f32),
            pltpu.VMEM(router_weight.shape, bf16),
            pltpu.VMEM(expert_ids.shape, jnp.int32),
            pltpu.VMEM((LANES, LANES), f32),
            pltpu.VMEM((2, chips, plan.sublanes, LANES), bf16),
            pltpu.VMEM((plan.tiles, width, 2 * LANES), bf16),
            pltpu.VMEM((plan.depth, width), bf16),
            pltpu.VMEM(shared_weights.shape, bf16),
            pltpu.VMEM((count * 2 * plan.half, width), bf16),
            pltpu.VMEM((count * 2 * plan.half, width), bf16),
            pltpu.VMEM((count * plan.half, width), bf16),
            pltpu.VMEM((2, hops, tok, width), bf16),
            pltpu.VMEM((2, hops, tok, width), bf16),
            pltpu.VMEM((plan.rows, plan.depth), bf16),
            pltpu.VMEM((plan.rows, 2 * LANES), f32),
            pltpu.VMEM((plan.rows, LANES), f32),
            dma((6,)),
            dma((plan.tiles, 2)),
            dma((2, hops, 3)),
            dma((2, hops, 3)),
            dma((chips, 5)),
            dma((chips, 5)),
            dma((count, 2)),
            dma((count, 2)),
            dma((2, hops, 4)),
            dma((2, hops, 4)),
        ],
        compiler_params=pltpu.CompilerParams(
            collective_id=0, has_side_effects=True, vmem_limit_bytes=64 * 1024 * 1024 - 65536
        ),
        name="moe_layer",
    )(
        hidden_state, norm_gain.reshape(1, width), router_weight, expert_ids, live_counts,
        routed_gate_up, routed_down, shared_weights,
    )
    return mixed, penalty


def fold_of(mesh):
    chips = mesh.shape["expert"]
    try:
        spots = [tuple(d.coords) for d in mesh.devices[0, :, 0].flat]
    except (AttributeError, TypeError, ValueError):
        spots = []
    if chips % 2 or chips < 4:
        return 1
    if len(spots) == chips:
        apart = sum(abs(a - b) for a, b in zip(spots[0], spots[2]))
        return 2 if apart == 1 else 1
    return 1


def solution(mesh):
    placed = (
        P(("groups", "expert", "sub"), None),
        P(),
        P(),
        P(("groups", "expert", "sub"), None),
        P(("groups", "expert", "sub")),
        P(("expert", "sub"), None, None),
        P(("expert", "sub"), None, None),
        P(None, None, "expert"),
    )
    return jax.shard_map(
        functools.partial(on_device, fold_of(mesh)),
        mesh=mesh,
        in_specs=placed,
        out_specs=(P(("groups", "expert", "sub"), None), P("groups")),
        check_vma=False,
    )
```

time: 100 us -> 84.1 us (0.84)
  matrix products: 21.5 us -> 0 us
  other arithmetic: 7.06 us -> 0 us
  local copies, waits for them, and re-layouts: 4.79 us -> 11.4 us
  Pallas kernels: 63.1 us -> 69.2 us
    dot_general x10 -> x0, matrix products: 21.5 us -> none  [the longest x1 6.2 us: on_device(): jnp.dot(rows, routed_gate_up[item], preferred_element_type=jnp.float32)]
    unnamed x19 -> x4, local copies, waits for them, and re-layouts: 4.14 us -> 11.4 us
    pallas_call x2 -> x1, Pallas kernels: 63.1 us -> 69.2 us  [on_device(): pl.pallas_call(functools.partial(layer_kernel, plan), out_shape=(jax.Shap...]
    reduce_sum x5 -> x0, other arithmetic: 3.9 us -> none  [the longest x1 1.3 us: on_device(): sums = jnp.sum(notes.reshape(devices, tok_rows, -1), axis=1)]
    convert_element_type x6 -> x0, other arithmetic: 2.32 us -> none  [the longest x1 1.08 us: normalize(): return (values * lax.rsqrt(spread + 1e-06) * norm_gain).astype(jnp.bfloat16)]
where the time goes in v1:
time: 84.1 us; the launch traced here: 83.7 us
  Pallas kernels  69.2 us (82%)
  local copies, waits for them, and re-layouts  11.4 us (14%)
  between operations  3.09 us (4%)
    pallas_call x1, Pallas kernels, on_device(): pl.pallas_call(functools.partial(layer_kernel, plan), out_shape=(jax.Shap...  69.2 us
    unnamed x4, local copies, waits for them, and re-layouts  11.4 us

profile of v1, /device:TPU:0, one launch (start us, length us, event | category | flops | bytes accessed | tf_op | source)
XLA Modules:
  0.0 83.7 jit_solution(7674732125200750813)
XLA Ops:
  1.3 1.4 %copy.11.ids_hbm = s32[64,6]{1,0:T(8,128)} copy(s32[64,6]{0,1:T(8,128)} %param.11) | data formatting | bytes 3072 | tf_op args[3]
  2.7 1.9 %copy.10.router_hbm = bf16[2048,16]{1,0:T(8,128)(2,1)} copy(bf16[2048,16]{0,1:T(8,128)(2,1)} %param.10) | data formatting | bytes 131072 | tf_op args[2]
  4.5 6.5 %copy.12.sh_hbm = bf16[3,2048,352]{2,1,0:T(8,128)(2,1)} copy(bf16[3,2048,352]{1,2,0:T(8,128)(2,1)} %param.15) | data formatting | bytes 8650752 | tf_op args[7]
  11.0 69.2 %moe_layer.1 = (bf16[64,2048]{1,0:T(8,128)(2,1)}, f32[1]{0:T(128)}) custom-call(bf16[64,2048]{1,0:T(8,128)(2,1)} %hid_hbm.1, f32[1,2048]{1,0:T(1,128)} %bitcast.1, bf16[2048,16]{1,0:T(8,128)(2,1)} %copy.10.router_hbm, s32[64,6]{1,0:T(8,128)} %copy.11.ids_hbm, s32[1]{0:T(128)S(6)} %copy.15.live_ref, bf16[1,2048,2816]{2,1,0:T(8,128)(2,1)} %gu_hbm.1, ...), custom_call_target="tpu_custom_call" | custom-call | tf_op jit(solution)/shard_map/moe_layer/pallas_call | solution.py:455
  80.2 1.7 %copy.16 = bf16[64,2048]{1,0:T(8,128)(2,1)} copy(bf16[64,2048]{1,0:T(8,128)(2,1)} %get-tuple-element.4) | data formatting | bytes 524288

commit v2 on v1

--- a/solution.py
+++ b/solution.py
@@ -10,6 +10,8 @@
 MESH = pl.DeviceIdType.MESH
 LANES = 128
 SLOTS = 5
+GATHER = (1, 2, 2, 4, 4, 5, 6, 7, 8, 9, 10, 11)
+SCATTER = (1, 1, 4, 4)
 
 
 def ring_place(chip, chips, fold):
@@ -98,31 +100,23 @@
             device_id=device, device_id_type=MESH,
         )
 
-    def gather_copy(way, hop, j):
-        cols = plan.cols(way) if hop == hops else pl.ds(0, width)
+    def gather_copy(way, hop, j, c):
+        cols, at = plan.cols(c), 2 * j + c
         src = x_all.at[plan.span(0, sign[way] * (hop - 1), j), cols]
         dst = x_all.at[plan.span(0, sign[way] * hop, j), cols]
-        return remote(src, dst, gs.at[way, hop - 1, j], gr.at[way, hop - 1, j], along[way])
+        return remote(src, dst, gs.at[way, hop - 1, at], gr.at[way, hop - 1, at], along[way])
 
     def note_copy(way, hop):
         src = notes.at[0, sign[way] * (hop - 1) % chips]
         dst = notes.at[0, sign[way] * hop % chips]
-        return remote(src, dst, gs.at[way, hop - 1, 2], gr.at[way, hop - 1, 2], along[way])
-
-    def peer_copies(k, j):
-        k = k % chips
-        parts = (0, 1) if k == hops else (2,)
-        made = []
-        for c in parts:
-            cols = pl.ds(0, width) if c == 2 else plan.cols(c)
-            at = 2 * j + c % 2
-            made.append(
-                remote(
-                    x_all.at[plan.span(0, k, j), cols], x_all.at[plan.span(1, k, j), cols],
-                    ps.at[k, at], pr.at[k, at], peer,
-                )
-            )
-        return made
+        return remote(src, dst, gs.at[way, hop - 1, 4], gr.at[way, hop - 1, 4], along[way])
+
+    def peer_copy(k, j, c):
+        k, cols, at = k % chips, plan.cols(c), 2 * j + c
+        return remote(
+            x_all.at[plan.span(0, k, j), cols], x_all.at[plan.span(1, k, j), cols],
+            ps.at[k, at], pr.at[k, at], peer,
+        )
 
     def peer_note(k):
         k = k % chips
@@ -147,6 +141,9 @@
             along[way],
         )
 
+    def side_of(way, part):
+        return way if part == 0 else 1 - way
+
     def ways_of(hop, c):
         return (c,) if hop == hops else (0, 1)
 
@@ -155,9 +152,25 @@
         pltpu.make_async_copy(gain_hbm, gain, in_sem.at[1]),
         pltpu.make_async_copy(router_hbm, router, in_sem.at[2]),
         pltpu.make_async_copy(ids_hbm, ids, in_sem.at[3]),
-        pltpu.make_async_copy(sh_hbm, stage, in_sem.at[4]),
+        pltpu.make_async_copy(sh_hbm.at[0], stage.at[0], in_sem.at[4]),
+        pltpu.make_async_copy(sh_hbm.at[1], stage.at[1], in_sem.at[5]),
     ]
-    down_load = pltpu.make_async_copy(dn_hbm.at[0], wd.at[pl.ds(0, plan.units)], in_sem.at[5])
+    down_loads = [pltpu.make_async_copy(dn_hbm.at[0], wd.at[pl.ds(0, plan.units)], in_sem.at[6])]
+    for i in range(plan.pairs):
+        down_loads.append(
+            pltpu.make_async_copy(
+                sh_hbm.at[2, pl.ds(pl.multiple_of((2 * i + sub) * LANES, LANES), LANES)],
+                wd.at[pl.ds(plan.units + i * LANES, LANES)], in_sem.at[7 + i],
+            )
+        )
+    for i, (at, wide) in enumerate(plan.rest):
+        n = plan.routed_tiles + plan.pairs + i
+        down_loads.append(
+            pltpu.make_async_copy(
+                sh_hbm.at[2, pl.ds(at, wide)], wd.at[pl.ds(n * LANES, wide)],
+                in_sem.at[7 + plan.pairs + i],
+            )
+        )
 
     def tile_loads(n):
         if n < plan.routed_tiles:
@@ -176,10 +189,12 @@
     for target in along + [peer]:
         pl.semaphore_signal(barrier, inc=1, device_id=target, device_id_type=MESH)
     small[4].start()
+    small[5].start()
     for n in range(tiles):
         for copy in tile_loads(n):
             copy.start()
-    down_load.start()
+    for copy in down_loads:
+        copy.start()
 
     small[0].wait()
     small[1].wait()
@@ -190,93 +205,97 @@
             values * lax.rsqrt(spread + 1e-06) * gain[...]
         ).astype(jnp.bfloat16)
     pl.semaphore_wait(barrier, 3)
-    for way in range(2):
-        if hops > 1 or way == 0:
-            gather_copy(way, 1, 0).start()
-    for copy in peer_copies(0, 0):
-        copy.start()
+    for part in range(2):
+        for way in range(2):
+            gather_copy(way, 1, 0, side_of(way, part)).start()
+    for c in range(2):
+        peer_copy(0, 0, c).start()
 
     small[2].wait()
     small[3].wait()
     experts = plan.experts
-    columns = lax.broadcasted_iota(jnp.int32, (half, experts), 1)
+    expert = lax.broadcasted_iota(jnp.int32, (experts, half), 0)
     square[...] = jnp.zeros_like(square)
-    load = jnp.zeros((1, experts), jnp.float32)
-    mass = jnp.zeros((1, experts), jnp.float32)
+    load = jnp.zeros((experts, 1), jnp.float32)
+    mass = jnp.zeros((experts, 1), jnp.float32)
+    named = ids[...]
     for j in range(2):
-        normed = x_all[plan.span(0, 0, j), :]
-        logits = jnp.dot(normed, router[...], preferred_element_type=jnp.float32)
+        logits = lax.dot_general(
+            router[...], x_all[plan.span(0, 0, j), :], (((1,), (1,)), ((), ())),
+            preferred_element_type=jnp.float32,
+        )
         probs = 1.0 / (1.0 + jnp.exp(-logits))
-        named = ids[pl.ds(j * half, half), :]
-        hot = jnp.zeros((half, experts), jnp.float32)
+        hot = jnp.zeros((experts, half), jnp.float32)
         for k in range(plan.choose):
-            hot = hot + jnp.where(named[:, k : k + 1] == columns, 1.0, 0.0)
-        token = lax.broadcasted_iota(jnp.int32, (half, experts), 0) + j * half
+            hot = hot + jnp.where(named[k : k + 1, j * half : (j + 1) * half] == expert, 1.0, 0.0)
+        token = lax.broadcasted_iota(jnp.int32, (experts, half), 1) + j * half
         live = jnp.where(token < live_ref[0], 1.0, 0.0)
         picked = hot * probs
-        weights = live * picked / jnp.sum(picked, axis=-1, keepdims=True)
-        square[pl.ds(j * half, half), pl.ds(0, experts)] = weights
-        load = load + jnp.sum(hot * live, axis=0, keepdims=True)
-        mass = mass + jnp.sum(probs * live, axis=0, keepdims=True)
-    square[pl.ds(tok, 1), pl.ds(0, experts)] = load
+        weights = live * picked / jnp.sum(picked, axis=0, keepdims=True)
+        square[pl.ds(0, experts), pl.ds(j * half, half)] = weights
+        load = load + jnp.sum(hot * live, axis=1, keepdims=True)
+        mass = mass + jnp.sum(probs * live, axis=1, keepdims=True)
+    square[pl.ds(0, experts), pl.ds(tok, 1)] = load
     for at in range(3):
         kept = mass.astype(jnp.bfloat16).astype(jnp.float32)
-        square[pl.ds(tok + 1 + at, 1), pl.ds(0, experts)] = kept
+        square[pl.ds(0, experts), pl.ds(tok + 1 + at, 1)] = kept
         mass = mass - kept
-    turned = jnp.transpose(square[...])
-    notes[0, 0] = turned[: plan.sublanes].astype(jnp.bfloat16)
+    notes[0, 0] = square[...].astype(jnp.bfloat16)
     for way in range(2):
-        if hops > 1 or way == 0:
-            note_copy(way, 1).start()
-        if hops > 1 or way == 1:
-            gather_copy(way, 1, 1).start()
+        note_copy(way, 1).start()
+    for way in range(2):
+        gather_copy(way, 1, 1, side_of(way, 0)).start()
     peer_note(0).start()
-    for copy in peer_copies(0, 1):
-        copy.start()
-
-    small[4].wait()
+    for c in range(2):
+        peer_copy(0, 1, c).start()
+
+    def arrive(hop, j, part):
+        for way in range(2):
+            k, c = sign[way] * hop, side_of(way, part)
+            gather_copy(way, hop, j, c).wait_recv()
+            if hop + 1 < hops or (hop + 1 == hops and part == 0):
+                gather_copy(way, hop + 1, j, c).start()
+            peer_copy(k, j, c).start()
+            if j == 0 and ((part == 1 and hop < hops) or (hop == hops and way == 0)):
+                note_copy(way, hop).wait_recv()
+                if hop + 1 < hops or (hop + 1 == hops and way == 0):
+                    note_copy(way, hop + 1).start()
+                peer_note(k).start()
+
+    arrive(1, 0, 0)
+    arrive(1, 0, 1)
+    for way in range(2):
+        gather_copy(way, 1, 1, side_of(way, 1)).start()
+
     for i in range(plan.pairs):
-        lanes = pl.ds(pl.multiple_of((2 * i + sub) * LANES, LANES), LANES)
         n = plan.routed_tiles + i
+        units = pl.ds(pl.multiple_of((2 * i + sub) * LANES, LANES), LANES)
         for side in range(2):
-            wt[n, :, pl.ds(side * LANES, LANES)] = stage[side, :, lanes]
-        wd[pl.ds(n * LANES, LANES), :] = jnp.transpose(stage[2, :, lanes])
+            if i == 0:
+                small[4 + side].wait()
+            wt[n, :, pl.ds(side * LANES, LANES)] = jnp.transpose(stage[side, units, :])
     for i, (at, wide) in enumerate(plan.rest):
         n = plan.routed_tiles + plan.pairs + i
         if wide < LANES:
             wt[n] = jnp.zeros_like(wt[n])
-        for side in range(2):
-            wt[n, :, pl.ds(side * LANES, wide)] = stage[side, :, pl.ds(at, wide)]
-        wd[pl.ds(n * LANES, wide), :] = jnp.transpose(stage[2, :, pl.ds(at, wide)])
-        if wide < LANES:
             wd[pl.ds(n * LANES + wide, LANES - wide), :] = jnp.zeros(
                 (LANES - wide, width), jnp.bfloat16
             )
+        for side in range(2):
+            if i == 0 and plan.pairs == 0:
+                small[4 + side].wait()
+            wt[n, :, pl.ds(side * LANES, wide)] = jnp.transpose(stage[side, pl.ds(at, wide), :])
 
     events = {}
 
     def at_slot(spot, event):
         events.setdefault(spot, []).append(event)
-
-    def arrive(hop, j):
-        for way in range(2):
-            k = sign[way] * hop
-            if j == 0 and (hop < hops or way == 0):
-                note_copy(way, hop).wait_recv()
-                if hop + 1 < hops or (hop + 1 == hops and way == 0):
-                    note_copy(way, hop + 1).start()
-                peer_note(k).start()
-            gather_copy(way, hop, j).wait_recv()
-            if hop + 1 <= hops:
-                gather_copy(way, hop + 1, j).start()
-            made = peer_copies(k, j)
-            (made[way] if hop == hops else made[0]).start()
 
     def ready(step):
         for i in range(plan.group):
             k, j = plan.order[step * plan.group + i]
-            for copy in peer_copies(k, j):
-                copy.wait_recv()
+            for c in range(2):
+                peer_copy(k, j, c).wait_recv()
             if j == 0:
                 peer_note(k).wait_recv()
             for r in range(2):
@@ -288,16 +307,23 @@
                 column = jnp.sum(jnp.where(row == lane, line, 0.0), axis=1, keepdims=True)
                 scale[pl.ds((2 * i + r) * half, half), :] = jnp.broadcast_to(column, (half, LANES))
 
-    arrivals = [(h, j) for h in range(1, hops + 1) for j in range(2)]
-    wanted = [0, 1, 3, 6, 8, 10, 10, 11]
+    arrivals = []
+    for hop in range(2, hops + 1):
+        arrivals.append((hop, 0, 0))
+        if hop > 2:
+            arrivals.append((hop - 2, 1, 1))
+        if hop < hops:
+            arrivals.append((hop, 0, 1))
+        arrivals.append((hop - 1, 1, 0))
+    arrivals += [(hops - 1, 1, 1), (hops, 1, 0)]
     spots = []
-    for i, (hop, j) in enumerate(arrivals):
+    for i, (hop, j, part) in enumerate(arrivals):
         due = SLOTS * min(plan.step_of(hop, j), plan.step_of(-hop, j))
-        spots.append(min(due, wanted[i] if i < len(wanted) else 2 * i))
+        spots.append(min(due, GATHER[i] if i < len(GATHER) else i))
     for i in reversed(range(len(spots) - 1)):
         spots[i] = min(spots[i], spots[i + 1])
-    for (hop, j), spot in zip(arrivals, spots):
-        at_slot(spot, functools.partial(arrive, hop, j))
+    for (hop, j, part), spot in zip(arrivals, spots):
+        at_slot(spot, functools.partial(arrive, hop, j, part))
     for step in range(plan.steps):
         at_slot(SLOTS * step, functools.partial(ready, step))
     quarter = 4
@@ -310,7 +336,8 @@
     for part in range(3):
         last = tiles if part == 2 else quarter * (part + 1)
         at_slot(part, functools.partial(loads, quarter * part, last))
-    at_slot(2, down_load.wait)
+    for copy in down_loads:
+        at_slot(2, copy.wait)
 
     def own_part(k, j, c):
         q = plan.index(k, j)
@@ -318,37 +345,36 @@
         value = y_all[plan.span(0, k, j), plan.cols(c)].astype(jnp.float32)
         return value + from_peer[pl.ds(q * half, half), plan.cols(c)].astype(jnp.float32)
 
-    def pass_on(hop, j):
-        for c in range(2):
-            shared = None
-            for way in ways_of(hop, c):
-                k = -sign[way] * hop
-                value = own_part(k, j, c)
-                if hop < hops and way in ways_of(hop + 1, c):
-                    sum_copy(way, hop + 1, j, c).wait_recv()
-                    spot = (way, hop, pl.ds(j * half, half), plan.cols(c))
-                    value = value + coming[spot].astype(jnp.float32)
-                spot = (way, hop - 1, pl.ds(j * half, half), plan.cols(c))
-                going[spot] = value.astype(going.dtype)
-                sum_copy(way, hop, j, c).start()
-
-    def finish(j):
-        for c in range(2):
-            value = own_part(0, j, c)
-            for way in ways_of(1, c):
-                sum_copy(way, 1, j, c).wait_recv()
-                spot = (way, 0, pl.ds(j * half, half), plan.cols(c))
+    def pass_on(hop, j, c):
+        for way in ways_of(hop, c):
+            value = own_part(-sign[way] * hop, j, c)
+            if hop < hops and way in ways_of(hop + 1, c):
+                sum_copy(way, hop + 1, j, c).wait_recv()
+                spot = (way, hop, pl.ds(j * half, half), plan.cols(c))
                 value = value + coming[spot].astype(jnp.float32)
-            out_ref[pl.ds(j * half, half), plan.cols(c)] = value.astype(out_ref.dtype)
-
-    first = [functools.partial(pass_on, h, 0) for h in range(hops, 0, -1)]
-    first.append(functools.partial(finish, 0))
-    second = [functools.partial(pass_on, h, 1) for h in range(hops, 0, -1)]
-    second.append(functools.partial(finish, 1))
-    spot = SLOTS * (plan.step_of(hops, 0) + 1) + 1
-    while EARLY and spot < SLOTS * plan.steps and len(first) > 1:
-        at_slot(spot, first.pop(0))
-        spot += 3
+            spot = (way, hop - 1, pl.ds(j * half, half), plan.cols(c))
+            going[spot] = value.astype(going.dtype)
+            sum_copy(way, hop, j, c).start()
+
+    def finish(j, c):
+        value = own_part(0, j, c)
+        for way in ways_of(1, c):
+            sum_copy(way, 1, j, c).wait_recv()
+            spot = (way, 0, pl.ds(j * half, half), plan.cols(c))
+            value = value + coming[spot].astype(jnp.float32)
+        out_ref[pl.ds(j * half, half), plan.cols(c)] = value.astype(out_ref.dtype)
+
+    def chain(j):
+        made = [
+            functools.partial(pass_on, h, j, c) for h in range(hops, 0, -1) for c in range(2)
+        ]
+        return made + [functools.partial(finish, j, c) for c in range(2)]
+
+    first, second = chain(0), chain(1)
+    base = SLOTS * (plan.step_of(hops, 0) + 1)
+    for at in SCATTER:
+        if base + at < SLOTS * plan.steps and first:
+            at_slot(base + at, first.pop(0))
 
     def run(t, slot):
         for step in range(plan.steps):
@@ -377,17 +403,25 @@
         rows = pl.ds(pl.multiple_of(t * plan.rows, plan.rows), plan.rows)
         run(t, 0)
         for n in range(tiles):
-            if n > 0:
-                activate(n - 1)
-            rbuf[...] = jnp.dot(x_all[rows, :], wt[n], preferred_element_type=jnp.float32)
+
+            @pl.when(t >= 0)
+            def _():
+                if n > 0:
+                    activate(n - 1)
+                rbuf[...] = jnp.dot(x_all[rows, :], wt[n], preferred_element_type=jnp.float32)
+
             if (n + 1) % quarter == 0 and (n + 1) // quarter < SLOTS - 1:
                 run(t, (n + 1) // quarter)
         activate(tiles - 1)
         for n in range(plan.downs):
             cols = pl.ds(n * 256, 256)
-            y_all[rows, cols] = jnp.dot(
-                act[...], wd[:, cols], preferred_element_type=jnp.float32
-            ).astype(jnp.bfloat16)
+
+            @pl.when(t >= 0)
+            def _():
+                y_all[rows, cols] = jnp.dot(
+                    act[...], wd[:, cols], preferred_element_type=jnp.float32
+                ).astype(jnp.bfloat16)
+
             if 2 * (n + 1) == plan.downs:
                 for i in range(plan.group):
                     part_copy(plan.group * t + i, 0).start()
@@ -399,8 +433,10 @@
     lax.fori_loop(0, plan.steps, step_body, 0)
 
     while first or second:
-        if second and len(second) >= len(first):
-            second.pop(0)()
+        if len(second) >= len(first):
+            for event in second[:2]:
+                event()
+            second = second[2:]
         else:
             first.pop(0)()
 
@@ -411,29 +447,25 @@
     mass = total[:, tok + 1 : tok + 2] + total[:, tok + 2 : tok + 3] + total[:, tok + 3 : tok + 4]
     every = float(tok * chips * 2)
     penalty = experts * jnp.sum(total[:, tok : tok + 1] * mass) / (plan.choose * every * every)
-    pen_ref[0] = penalty
+    pen_ref[...] = jnp.full((8, LANES), penalty, jnp.float32)
 
     for hop in range(1, hops + 1):
         for way in range(2):
-            for j in range(2):
-                gather_copy(way, hop, j).wait_send()
             if hop < hops or way == 0:
                 note_copy(way, hop).wait_send()
             for j in range(2):
                 for c in range(2):
                     if way in ways_of(hop, c):
+                        gather_copy(way, hop, j, c).wait_send()
                         sum_copy(way, hop, j, c).wait_send()
     for k in range(chips):
         peer_note(k).wait_send()
         for j in range(2):
-            for copy in peer_copies(k, j):
-                copy.wait_send()
+            for c in range(2):
+                peer_copy(k, j, c).wait_send()
     for q in range(len(plan.order)):
         for c in range(2):
             part_copy(q, c).wait_send()
-
-
-EARLY = True
 
 
 def on_device(
@@ -455,24 +487,24 @@
     mixed, penalty = pl.pallas_call(
         functools.partial(layer_kernel, plan),
         out_shape=(
-            jax.ShapeDtypeStruct((tok, width), bf16),
-            jax.ShapeDtypeStruct((1,), f32),
+            pltpu.VMEM((tok, width), bf16),
+            pltpu.VMEM((8, LANES), f32),
         ),
         in_specs=[hbm] * 4 + [pl.BlockSpec(memory_space=pltpu.SMEM)] + [hbm] * 3,
         out_specs=(
             pl.BlockSpec(memory_space=pltpu.VMEM),
-            pl.BlockSpec(memory_space=pltpu.SMEM),
+            pl.BlockSpec(memory_space=pltpu.VMEM),
         ),
         scratch_shapes=[
             pltpu.VMEM((tok, width), bf16),
             pltpu.VMEM((1, width), f32),
-            pltpu.VMEM(router_weight.shape, bf16),
-            pltpu.VMEM(expert_ids.shape, jnp.int32),
-            pltpu.VMEM((LANES, LANES), f32),
+            pltpu.VMEM(router_weight.shape[::-1], bf16),
+            pltpu.VMEM(expert_ids.shape[::-1], jnp.int32),
+            pltpu.VMEM((plan.sublanes, LANES), f32),
             pltpu.VMEM((2, chips, plan.sublanes, LANES), bf16),
             pltpu.VMEM((plan.tiles, width, 2 * LANES), bf16),
             pltpu.VMEM((plan.depth, width), bf16),
-            pltpu.VMEM(shared_weights.shape, bf16),
+            pltpu.VMEM((2, shared, width), bf16),
             pltpu.VMEM((count * 2 * plan.half, width), bf16),
             pltpu.VMEM((count * 2 * plan.half, width), bf16),
             pltpu.VMEM((count * plan.half, width), bf16),
@@ -481,10 +513,10 @@
             pltpu.VMEM((plan.rows, plan.depth), bf16),
             pltpu.VMEM((plan.rows, 2 * LANES), f32),
             pltpu.VMEM((plan.rows, LANES), f32),
-            dma((6,)),
+            dma((7 + plan.pairs + len(plan.rest),)),
             dma((plan.tiles, 2)),
-            dma((2, hops, 3)),
-            dma((2, hops, 3)),
+            dma((2, hops, 5)),
+            dma((2, hops, 5)),
             dma((chips, 5)),
             dma((chips, 5)),
             dma((count, 2)),
@@ -493,14 +525,14 @@
             dma((2, hops, 4)),
         ],
         compiler_params=pltpu.CompilerParams(
-            collective_id=0, has_side_effects=True, vmem_limit_bytes=64 * 1024 * 1024 - 65536
+            collective_id=0, has_side_effects=True, vmem_limit_bytes=127 * 512 * 1024
         ),
         name="moe_layer",
     )(
-        hidden_state, norm_gain.reshape(1, width), router_weight, expert_ids, live_counts,
-        routed_gate_up, routed_down, shared_weights,
+        hidden_state, norm_gain.reshape(1, width), router_weight.T, expert_ids.T, live_counts,
+        routed_gate_up, routed_down, jnp.swapaxes(shared_weights, 1, 2),
     )
-    return mixed, penalty
+    return mixed, penalty[0, :1]
 
 
 def fold_of(mesh):

time: 84.1 us -> 68.1 us (0.81)
  local copies, waits for them, and re-layouts: 11.4 us -> 1.22 us
  Pallas kernels: 69.2 us -> 65.5 us
  between operations: 3.09 us -> 1.29 us
    unnamed x4 -> x1, local copies, waits for them, and re-layouts: 11.4 us -> 0.7 us
    pallas_call x1, Pallas kernels: 69.2 us -> 65.5 us  [on_device(): pl.pallas_call(functools.partial(layer_kernel, plan), out_shape=(pltpu.VM...]
where the time goes in v2:
time: 68.1 us; the launch traced here: 68 us
  Pallas kernels  65.5 us (96%)
  between operations  1.29 us (2%)
  local copies, waits for them, and re-layouts  1.22 us (2%)
    pallas_call x1, Pallas kernels, on_device(): pl.pallas_call(functools.partial(layer_kernel, plan), out_shape=(pltpu.VM...  65.5 us

profile of v2, /device:TPU:0, one launch (start us, length us, event | category | flops | bytes accessed | tf_op | source)
XLA Modules:
  0.0 68.0 jit_solution(10865502295092155193)
XLA Ops:
  1.3 65.5 %moe_layer.1 = (bf16[64,2048]{1,0:T(8,128)(2,1)S(1)}, f32[8,128]{1,0:T(8,128)S(1)}) custom-call(bf16[64,2048]{1,0:T(8,128)(2,1)} %hid_hbm.1, f32[1,2048]{1,0:T(1,128)} %bitcast.7, bf16[16,2048]{1,0:T(8,128)(2,1)} %bitcast.6, s32[6,64]{1,0:T(8,128)} %bitcast.8, s32[1]{0:T(128)S(6)} %copy.12.live_ref, bf16[1,2048,2816]{2,1,0:T(8,128)(2,1)} %gu_hbm.1, ...), custom_call_target="tpu_custom_call" | custom-call | tf_op jit(solution)/shard_map/moe_layer/pallas_call | solution.py:487
  66.7 0.5 slice.3
  67.3 0.7 %copy.11 = bf16[64,2048]{1,0:T(8,128)(2,1)} copy(bf16[64,2048]{1,0:T(8,128)(2,1)S(1)} %get-tuple-element.6) | data formatting | bytes 524288

commit v3 on v2

--- a/solution.py
+++ b/solution.py
@@ -10,7 +10,7 @@
 MESH = pl.DeviceIdType.MESH
 LANES = 128
 SLOTS = 5
-GATHER = (1, 2, 2, 4, 4, 5, 6, 7, 8, 9, 10, 11)
+GATHER = (1, 2, 2, 4, 4, 5, 6, 7, 8, 9, 12, 13)
 SCATTER = (1, 1, 4, 4)
 
 
@@ -432,22 +432,26 @@
 
     lax.fori_loop(0, plan.steps, step_body, 0)
 
+    def totals():
+        total = jnp.zeros((plan.sublanes, LANES), jnp.float32)
+        for r in range(2):
+            for k in range(chips):
+                total = total + notes[r, k].astype(jnp.float32)
+        mass = total[:, tok + 1 : tok + 2] + total[:, tok + 2 : tok + 3] + total[:, tok + 3 : tok + 4]
+        every = float(tok * chips * 2)
+        penalty = experts * jnp.sum(total[:, tok : tok + 1] * mass) / (plan.choose * every * every)
+        pen_ref[...] = jnp.full((8, LANES), penalty, jnp.float32)
+
+    rounds = 0
     while first or second:
-        if len(second) >= len(first):
-            for event in second[:2]:
-                event()
-            second = second[2:]
-        else:
+        if len(first) % 2:
             first.pop(0)()
-
-    total = jnp.zeros((plan.sublanes, LANES), jnp.float32)
-    for r in range(2):
-        for k in range(chips):
-            total = total + notes[r, k].astype(jnp.float32)
-    mass = total[:, tok + 1 : tok + 2] + total[:, tok + 2 : tok + 3] + total[:, tok + 3 : tok + 4]
-    every = float(tok * chips * 2)
-    penalty = experts * jnp.sum(total[:, tok : tok + 1] * mass) / (plan.choose * every * every)
-    pen_ref[...] = jnp.full((8, LANES), penalty, jnp.float32)
+        for event in second[:2] + first[:2]:
+            event()
+        second, first = second[2:], first[2:]
+        rounds += 1
+        if rounds == 2:
+            totals()
 
     for hop in range(1, hops + 1):
         for way in range(2):

time: 68.1 us -> 66.8 us (0.981)
  Pallas kernels: 65.5 us -> 64.2 us
    pallas_call x1, Pallas kernels: 65.5 us -> 64.2 us  [on_device(): pl.pallas_call(functools.partial(layer_kernel, plan), out_shape=(pltpu.VM...]
where the time goes in v3:
time: 66.8 us; the launch traced here: 66.7 us
  Pallas kernels  64.2 us (96%)
  between operations  1.29 us (2%)
  local copies, waits for them, and re-layouts  1.22 us (2%)
    pallas_call x1, Pallas kernels, on_device(): pl.pallas_call(functools.partial(layer_kernel, plan), out_shape=(pltpu.VM...  64.2 us

profile of v3, /device:TPU:0, one launch (start us, length us, event | category | flops | bytes accessed | tf_op | source)
XLA Modules:
  0.0 66.7 jit_solution(9366716269297709668)
XLA Ops:
  1.3 64.2 %moe_layer.1 = (bf16[64,2048]{1,0:T(8,128)(2,1)S(1)}, f32[8,128]{1,0:T(8,128)S(1)}) custom-call(bf16[64,2048]{1,0:T(8,128)(2,1)} %hid_hbm.1, f32[1,2048]{1,0:T(1,128)} %bitcast.7, bf16[16,2048]{1,0:T(8,128)(2,1)} %bitcast.6, s32[6,64]{1,0:T(8,128)} %bitcast.8, s32[1]{0:T(128)S(6)} %copy.12.live_ref, bf16[1,2048,2816]{2,1,0:T(8,128)(2,1)} %gu_hbm.1, ...), custom_call_target="tpu_custom_call" | custom-call | tf_op jit(solution)/shard_map/moe_layer/pallas_call | solution.py:491
  65.4 0.5 slice.3
  66.0 0.7 %copy.11 = bf16[64,2048]{1,0:T(8,128)(2,1)} copy(bf16[64,2048]{1,0:T(8,128)(2,1)S(1)} %get-tuple-element.6) | data formatting | bytes 524288
